TPU v7x, 32 devices: a whole 2x2x4 slice. The times are simulated.
32 devices in a mesh: grp: 2 (over x), shard: 16 (over z, y, core).
Axes of the slice: x: 2, y: 2, z: 4, core: 2. Of those that a mesh axis runs over, the one named last changes fastest.
Arguments:
- window: bfloat16 [32, 4096], P('grp'), may hold values from -6 to 6
- weight: bfloat16 [11008, 4096], P('shard'), may hold values from -0.09375 to 0.09375
- factor_a: bfloat16 [64, 4, 4096], P(('grp', 'shard')), may hold values from -6 to 6
- factor_b: bfloat16 [64, 4, 11008], P(('grp', 'shard')), may hold values from -6 to 6
- fitness: float32 [64], P(('grp', 'shard')), may hold values from -4 to 4
Outputs:
- perturbed: bfloat16 [11008, 1024], P('shard', 'grp')
- update: float32 [11008, 4096], P('shard', 'grp')
All inputs are finite; a program needn't handle non-finite values.
Results may differ from a plain program's by a relative error of at most 0.0029.
Values may be sent and summed in bfloat16 or wider, within the bound.
A program may use at most 64 MiB of HBM per device.

v0:
```python
import math

import jax
import jax.numpy as jnp
from jax import lax
from jax.sharding import PartitionSpec as P


def contract(left_rows, right_rows):
    return lax.dot_general(
        left_rows, right_rows, (((0,), (0,)), ((), ())), preferred_element_type=jnp.float32
    )


def local(window, weight, factor_a, factor_b, fitness):
    model_width = window.shape[1]
    cand_dev, factor_rank, _ = factor_a.shape
    shard_count = lax.axis_size("shard")
    total_cands = cand_dev * lax.axis_size("grp") * shard_count
    perturb = 0.25 / math.sqrt(model_width)
    step_scale = 0.5 / math.sqrt(total_cands)
    base_out = lax.dot_general(
        weight, window, (((1,), (1,)), ((), ())), preferred_element_type=jnp.float32
    )
    projected = jnp.einsum("td,crd->crt", window, factor_a, preferred_element_type=jnp.float32)
    projected_all, fitness_all = (
        lax.all_gather(projected, "shard", axis=0, tiled=True),
        lax.all_gather(fitness, "shard", axis=0, tiled=True),
    )
    columns = lax.all_to_all(factor_b, "shard", split_axis=2, concat_axis=0, tiled=True)
    col_width = columns.shape[2]
    low_rank = jnp.einsum(
        "crt,crf->fct", projected_all, columns.astype(jnp.float32), precision=lax.Precision.HIGHEST
    )
    perturbed = (
        (base_out[:, None, :] + perturb * low_rank).astype(jnp.bfloat16).reshape(col_width, -1)
    )
    weighted = (fitness_all[:, None, None] * columns.astype(jnp.float32)).astype(jnp.bfloat16)
    exchanged = lax.all_to_all(factor_a, "grp", split_axis=2, concat_axis=0, tiled=True)
    weighted_four = weighted.reshape(shard_count, cand_dev, factor_rank, col_width)
    weighted_flat = lax.all_gather(weighted_four, "grp", axis=1, tiled=True).reshape(-1, col_width)
    owned_width = exchanged.shape[2]
    block_width = owned_width // 4
    update_parts = []
    for part_index in range(4):
        factor_slab = exchanged[:, :, part_index * block_width : (part_index + 1) * block_width]
        gathered = lax.all_gather(factor_slab, "shard", axis=0, tiled=True)
        update_parts.append(contract(weighted_flat, gathered.reshape(-1, block_width)))
    update = jnp.concatenate(update_parts, 1) * step_scale
    return (perturbed, update)


def solution(mesh):
    in_specs = (
        P("grp", None),
        P("shard", None),
        P(("grp", "shard"), None, None),
        P(("grp", "shard"), None, None),
        P(("grp", "shard")),
    )
    out_specs = (P("shard", "grp"), P("shard", "grp"))
    return jax.shard_map(local, mesh=mesh, in_specs=in_specs, out_specs=out_specs, check_vma=False)
```

profile of v0, /device:TPU:0, one launch (start us, length us, event | category | flops | bytes accessed | tf_op | source)
XLA Modules:
  0.0 226.9 jit_solution(7585882269689568177)
XLA Ops:
  0.6 4.4 %copy.14 = bf16[2,4,4096]{1,0,2:T(2,128)(2,1)S(1)} copy(bf16[2,4,4096]{2,1,0:T(4,128)(2,1)} %param.7) | data formatting | bytes 131072 | tf_op args[2]
  5.1 4.6 %reshape.41 = bf16[2,2,8192]{2,1,0:T(2,128)(2,1)} reshape(bf16[4096,2,4]{2,1,0:T(2,128)(2,1)S(1)} %bitcast.38) | data formatting | bytes 131072
  9.7 4.2 %all-to-all-start.1 = ((bf16[2,2,8192]{2,1,0:T(2,128)(2,1)}), bf16[2,2,8192]{2,1,0:T(2,128)(2,1)S(1)}, u32[]{:S(2)}, u32[]{:S(2)}) async-start(bf16[2,2,8192]{2,1,0:T(2,128)(2,1)} %reshape.41), calls=%async_computation.1 | async-start | bytes 131072 | tf_op jit(solution)/shard_map/all_to_all | solution.py:39
  13.9 4.8 %fusion.4 = f32[688,16]{0,1:T(8,128)} fusion(bf16[688,4096]{1,0:T(8,128)(2,1)} %param.6, bf16[16,4096]{1,0:T(8,128)(2,1)S(1)} %copy-done), kind=kOutput, calls=%fused_computation.7 | convolution fusion | flops 90177536 | bytes 5811200 | tf_op jit(solution)/shard_map/dot_general | solution.py:22
  19.0 9.0 %copy.12 = bf16[2,4,11008]{1,0,2:T(2,128)(2,1)} copy(bf16[2,4,11008]{2,1,0:T(4,128)(2,1)S(1)} %copy-done.3) | data formatting | bytes 352256 | tf_op args[3]
  28.0 15.1 %reshape.39 = bf16[16,2,2752]{2,1,0:T(2,128)(2,1)} reshape(bf16[11008,2,4]{2,1,0:T(2,128)(2,1)} %bitcast.36) | data formatting | bytes 352256
  44.5 34.0 %all-reduce = f32[32]{0:T(128)S(1)} all-reduce(f32[32]{0:T(128)S(1)} %dynamic-update-slice), channel_id=1, replica_groups=mesh['grp'=2,'shard'=16] {'shard'}, use_global_device_ids=true, to_apply=%add | all-reduce | flops 32 | bytes 256
  78.7 18.7 %all_gather.21 = f32[32,4,16]{2,1,0:T(4,128)} all-gather(f32[2,4,16]{2,1,0:T(4,128)S(1)} %fusion.1), channel_id=1, replica_groups=mesh['grp'=2,'shard'=16] {'shard'}, dimensions={0}, use_global_device_ids=true | all-gather | bytes 8704 | tf_op jit(solution)/shard_map/all_gather | solution.py:27
  97.4 3.5 %all-to-all-start = ((bf16[16,2,2752]{2,1,0:T(2,128)(2,1)}), bf16[16,2,2752]{2,1,0:T(2,128)(2,1)S(1)}, u32[]{:S(2)}, u32[]{:S(2)}) async-start(bf16[16,2,2752]{2,1,0:T(2,128)(2,1)} %reshape.39), calls=%async_computation | async-start | bytes 360448 | tf_op jit(solution)/shard_map/all_to_all | solution.py:30
  100.9 4.5 %reshape.42 = bf16[4096,2,4]{2,1,0:T(2,128)(2,1)S(1)} reshape(bf16[2,2,8192]{2,1,0:T(2,128)(2,1)S(1)} %all-to-all-done.1) | data formatting | bytes 131072
  105.4 1.4 copy.15
  106.9 22.4 %all_gather.24 = bf16[64,4,512]{2,1,0:T(4,128)(2,1)S(1)} all-gather(bf16[4,4,512]{2,1,0:T(4,128)(2,1)S(1)} %get-tuple-element.8), channel_id=1, replica_groups=mesh['grp'=2,'shard'=16] {'shard'}, dimensions={0}, use_global_device_ids=true | all-gather | bytes 278528 | tf_op jit(solution)/shard_map/all_gather | solution.py:47
  129.3 18.2 %all_gather.25 = bf16[64,4,512]{2,1,0:T(4,128)(2,1)S(1)} all-gather(bf16[4,4,512]{2,1,0:T(4,128)(2,1)S(1)} %get-tuple-element.11), channel_id=1, replica_groups=mesh['grp'=2,'shard'=16] {'shard'}, dimensions={0}, use_global_device_ids=true | all-gather | bytes 278528 | tf_op jit(solution)/shard_map/all_gather | solution.py:47
  148.2 19.5 %all_gather.26 = bf16[64,4,512]{2,1,0:T(4,128)(2,1)S(1)} all-gather(bf16[4,4,512]{2,1,0:T(4,128)(2,1)S(1)} %get-tuple-element.10), channel_id=1, replica_groups=mesh['grp'=2,'shard'=16] {'shard'}, dimensions={0}, use_global_device_ids=true | all-gather | bytes 278528 | tf_op jit(solution)/shard_map/all_gather | solution.py:47
  168.5 18.1 %all_gather.27 = bf16[64,4,512]{2,1,0:T(4,128)(2,1)S(1)} all-gather(bf16[4,4,512]{2,1,0:T(4,128)(2,1)S(1)} %get-tuple-element.9), channel_id=1, replica_groups=mesh['grp'=2,'shard'=16] {'shard'}, dimensions={0}, use_global_device_ids=true | all-gather | bytes 278528 | tf_op jit(solution)/shard_map/all_gather | solution.py:47
  187.4 7.4 %reshape.40 = bf16[11008,2,4]{2,1,0:T(2,128)(2,1)} reshape(bf16[16,2,2752]{2,1,0:T(2,128)(2,1)S(1)} %all-to-all-done) | data formatting | bytes 352256
  194.8 10.7 %copy.13 = bf16[2,4,16,688]{3,1,0,2:T(4,128)(2,1)S(1)} copy(bf16[2,4,16,688]{1,0,3,2:T(2,128)(2,1)} %bitcast.35) | data formatting | bytes 352256 | tf_op jit(solution)/shard_map/all_to_all | solution.py:30
  205.6 8.0 %all_gather.23 = bf16[16,4,4,688]{3,2,1,0:T(4,128)(2,1)S(1)} all-gather(bf16[16,2,4,688]{3,2,1,0:T(4,128)(2,1)S(1)} %multiply_convert_fusion), channel_id=1, replica_groups=mesh['grp'=2,'shard'=16] {'grp'}, dimensions={1}, use_global_device_ids=true | all-gather | bytes 528384 | tf_op jit(solution)/shard_map/all_gather | solution.py:41
  214.2 1.4 fusion.6
  215.6 1.5 fusion.7
  217.1 1.5 fusion.8
  218.5 1.8 fusion
  220.3 2.2 copy.16
  222.6 4.4 %maximum_multiply_fusion = f32[688,2048]{1,0:T(8,128)} fusion(f32[688,512]{1,0:T(8,128)} %fusion.8, f32[688,512]{1,0:T(8,128)} %fusion.7, f32[688,512]{1,0:T(8,128)S(1)} %fusion.6, f32[688,512]{1,0:T(8,128)S(1)} %fusion.5), kind=kLoop, calls=%fused_computation | loop fusion | flops 5636096 | bytes 11272192 | tf_op jit(solution)/shard_map/mul | solution.py:49
  (33 shorter events, 4.3 us)
Async XLA Ops:
  0.6 13.3 %copy-start = (bf16[16,4096]{1,0:T(8,128)(2,1)S(1)}, bf16[16,4096]{1,0:T(8,128)(2,1)}, u32[]{:S(2)}) copy-start(bf16[16,4096]{1,0:T(8,128)(2,1)} %param.5) | copy-start | bytes 393220
  9.7 87.7 %all-to-all-start.1 = ((bf16[2,2,8192]{2,1,0:T(2,128)(2,1)}), bf16[2,2,8192]{2,1,0:T(2,128)(2,1)S(1)}, u32[]{:S(2)}, u32[]{:S(2)}) async-start(bf16[2,2,8192]{2,1,0:T(2,128)(2,1)} %reshape.41), calls=%async_computation.1 | async-start | bytes 131072 | tf_op jit(solution)/shard_map/all_to_all | solution.py:39
  13.9 4.8 %copy-start.4 = (bf16[2,4,4096]{2,1,0:T(4,128)(2,1)S(1)}, bf16[2,4,4096]{2,1,0:T(4,128)(2,1)}, u32[]{:S(2)}) copy-start(bf16[2,4,4096]{2,1,0:T(4,128)(2,1)} %param.7) | copy-start | bytes 196612
  13.9 5.1 %copy-start.3 = (bf16[2,4,11008]{2,1,0:T(4,128)(2,1)S(1)}, bf16[2,4,11008]{2,1,0:T(4,128)(2,1)}, u32[]{:S(2)}) copy-start(bf16[2,4,11008]{2,1,0:T(4,128)(2,1)} %param.8) | copy-start | bytes 528388
  28.0 15.1 %copy-start.8 = (u32[32]{0:T(128)S(1)}, u32[32]{0:T(128)}, u32[]{:S(2)}) copy-start(u32[32]{0:T(128)} %constant.9) | copy-start | bytes 388
  28.0 16.3 %copy-start.7 = (f32[2]{0:T(128)S(1)}, f32[2]{0:T(128)}, u32[]{:S(2)}) copy-start(f32[2]{0:T(128)} %param.9) | copy-start | bytes 28
  97.4 90.0 %all-to-all-start = ((bf16[16,2,2752]{2,1,0:T(2,128)(2,1)}), bf16[16,2,2752]{2,1,0:T(2,128)(2,1)S(1)}, u32[]{:S(2)}, u32[]{:S(2)}) async-start(bf16[16,2,2752]{2,1,0:T(2,128)(2,1)} %reshape.39), calls=%async_computation | async-start | bytes 360448 | tf_op jit(solution)/shard_map/all_to_all | solution.py:30
  213.8 1.8 copy-start.1
  214.2 2.9 %copy-start.2 = (bf16[256,512]{1,0:T(8,128)(2,1)S(1)}, bf16[256,512]{1,0:T(8,128)(2,1)}, u32[]{:S(2)}) copy-start(bf16[256,512]{1,0:T(8,128)(2,1)} %reshape.32) | copy-start | bytes 786436
  215.6 3.0 %copy-start.5 = (f32[32,4,16]{2,1,0:T(4,128)S(1)}, f32[32,4,16]{2,1,0:T(4,128)}, u32[]{:S(2)}) copy-start(f32[32,4,16]{2,1,0:T(4,128)} %all_gather.21) | copy-start | bytes 24580
  215.6 3.0 %copy-start.6 = (f32[688,16]{0,1:T(8,128)S(1)}, f32[688,16]{0,1:T(8,128)}, u32[]{:S(2)}) copy-start(f32[688,16]{0,1:T(8,128)} %fusion.4) | copy-start | bytes 132100
where the time goes:
time: 228 us; the launch traced here: 227 us
  blocking collectives  139 us (61%)
  local copies, waits for them, and re-layouts  62.9 us (28%)
  matrix products  11.5 us (5%)
  starting transfers between devices  7.75 us (3%)
  other arithmetic  4.51 us (2%)
    all_gather x4, blocking collectives, local(): gathered = lax.all_gather(factor_slab, 'shard', axis=0, tiled=True)  78.1 us
    unnamed x28, local copies, waits for them, and re-layouts  48.1 us
    unnamed x1, blocking collectives  34 us
    all_gather x1, blocking collectives, local(): lax.all_gather(projected, 'shard', axis=0, tiled=True)  18.7 us
    all_to_all x1, local copies, waits for them, and re-layouts, local(): lax.all_to_all(factor_b, 'shard', split_axis=2, concat_axis=0, tiled=True)  10.7 us
    all_gather x1, blocking collectives, local(): lax.all_gather(weighted_four, 'grp', axis=1, tiled=True)  8 us
    dot_general x1, matrix products, local(): lax.dot_general(weight, window, (((1,), (1,)), ((), ())), preferred_eleme...  4.83 us
    dot_general x4, matrix products, contract(): lax.dot_general(left_rows, right_rows, (((0,), (0,)), ((), ())), preferre...  4.67 us
  transfers between devices with their start and end apart: 2, of which 0 were waited for; matrix products, arithmetic and copies ran while one was open for 17% of the time, Pallas kernels for 0%

commit v1 on v0

v1 whole, which is shorter than its diff:
```python
import functools
import math

import jax
import jax.numpy as jnp
from jax import lax
from jax.experimental import pallas as pl
from jax.experimental.pallas import tpu as pltpu
from jax.sharding import PartitionSpec as P

MESH = pl.DeviceIdType.MESH
F32 = jnp.float32
BF16 = jnp.bfloat16
ROW_CHUNK = 128


def dot_rows(left, right):
    return lax.dot_general(left, right, (((1,), (1,)), ((), ())), preferred_element_type=F32)


def dot_cols(left, right):
    return lax.dot_general(left, right, (((0,), (0,)), ((), ())), preferred_element_type=F32)


def exchange_kernel(
    n_grp, n_shard, fit_ref, win_ref, a_ref, b_ref, weight_ref,
    a_all, b_all, small_all, base_ref,
    small, weight, w_sem, b_send, b_recv, s_send, s_recv,
    a_send, a_send2, a_send3, a_recv1, a_recv2, a_recv3,
):
    depth = n_shard // 4
    count = n_grp * n_shard
    line = n_grp * depth
    grp = lax.axis_index("grp")
    shard = lax.axis_index("shard")
    core = shard % 2
    y = (shard // 2) % 2
    z = shard // 4
    me = grp * n_shard + shard
    own = core * (2 * line) + y * line + grp * depth + z
    half = a_all.shape[2]
    rows = b_ref.shape[1]
    ff = weight_ref.shape[0]
    cand_dev = fit_ref.shape[0]
    rank = rows // cand_dev
    tok = win_ref.shape[0]

    chunks = [(lo, min(ROW_CHUNK, ff - lo)) for lo in range(0, ff, ROW_CHUNK)]
    loads = [
        pltpu.make_async_copy(
            weight_ref.at[pl.ds(lo, size)], weight.at[pl.ds(lo, size)], w_sem.at[i]
        )
        for i, (lo, size) in enumerate(chunks)
    ]
    for load in loads:
        load.start()

    barrier = pltpu.get_barrier_semaphore()

    def greet(i, carry):
        t = (me + i) % count
        pl.semaphore_signal(
            barrier, inc=1, device_id=(t // n_shard, t % n_shard), device_id_type=MESH
        )
        return carry

    lax.fori_loop(1, count, greet, 0)
    pl.semaphore_wait(barrier, count - 1)

    def place(i):
        return (grp + i // depth) % n_grp, (z + i) % depth

    def origin(i):
        return (grp + n_grp - i // depth) % n_grp, (z + depth - i % depth) % depth

    def a_source(g):
        return a_ref.at[:, pl.ds(pl.multiple_of(g * half, half), half)]

    def send_a(i, carry):
        g, zz = place(i)
        pltpu.make_async_remote_copy(
            src_ref=a_source(g),
            dst_ref=a_all.at[own],
            send_sem=a_send,
            recv_sem=a_recv1.at[i],
            device_id=(g, zz * 4 + y * 2 + core),
            device_id_type=MESH,
        ).start()
        return carry

    lax.fori_loop(1, line, send_a, 0)
    pltpu.make_async_copy(a_source(grp), a_all.at[own], a_recv1.at[0]).start()

    def send_b(i, carry):
        t = (me + i) % count
        pltpu.make_async_remote_copy(
            src_ref=b_ref.at[t % n_shard],
            dst_ref=b_all.at[own],
            send_sem=b_send,
            recv_sem=b_recv,
            device_id=(t // n_shard, t % n_shard),
            device_id_type=MESH,
        ).start()
        return carry

    lax.fori_loop(1, count, send_b, 0)
    pltpu.make_async_copy(b_ref.at[shard], b_all.at[own], b_recv).start()

    win = win_ref[...]
    projected = dot_rows(a_ref[...], win)
    row = lax.broadcasted_iota(jnp.int32, (rows, tok), 0)
    fit = jnp.zeros((rows, tok), F32)
    for j in range(cand_dev):
        fit = jnp.where(row // rank == j, fit_ref[j], fit)
    small[...] = jnp.zeros(small.shape, F32)
    small[:, :tok] = projected
    small[:, tok : 2 * tok] = fit

    def forward_y(i):
        g, zz = origin(i)
        slot = core * (2 * line) + y * line + g * depth + zz
        return pltpu.make_async_remote_copy(
            src_ref=a_all.at[slot],
            dst_ref=a_all.at[slot],
            send_sem=a_send2,
            recv_sem=a_recv2.at[i],
            device_id=(grp, z * 4 + (1 - y) * 2 + core),
            device_id_type=MESH,
        )

    def forward_core(i, yy):
        g, zz = origin(i)
        slot = core * (2 * line) + yy * line + g * depth + zz
        return pltpu.make_async_remote_copy(
            src_ref=a_all.at[slot],
            dst_ref=a_all.at[slot],
            send_sem=a_send3,
            recv_sem=a_recv3,
            device_id=(grp, z * 4 + y * 2 + (1 - core)),
            device_id_type=MESH,
        )

    def relay(i, carry):
        pltpu.make_async_copy(a_all.at[0], a_all.at[0], a_recv1.at[i]).wait()
        forward_y(i).start()
        forward_core(i, y).start()
        return carry

    def base_chunk(i):
        lo, size = chunks[i]
        loads[i].wait()
        win3 = jnp.concatenate([win, win, win], axis=0)
        base = dot_rows(weight[pl.ds(lo, size)], win3)
        high = base.astype(BF16)
        rest = base - high.astype(F32)
        mid = rest.astype(BF16)
        low = (rest - mid.astype(F32)).astype(BF16)
        part = lax.broadcasted_iota(jnp.int32, base.shape, 1) // tok
        terms = jnp.where(
            part == 0, high.astype(F32), jnp.where(part == 1, mid.astype(F32), low.astype(F32))
        )
        base_ref[pl.ds(lo, size), :] = terms.astype(BF16)

    lax.fori_loop(0, 1, relay, 0)
    base_chunk(0)

    def send_small(i, carry):
        t = (me + i) % count
        pltpu.make_async_remote_copy(
            src_ref=small,
            dst_ref=small_all.at[own],
            send_sem=s_send,
            recv_sem=s_recv,
            device_id=(t // n_shard, t % n_shard),
            device_id_type=MESH,
        ).start()
        return carry

    lax.fori_loop(1, count, send_small, 0)
    pltpu.make_async_copy(small, small_all.at[own], s_recv).start()
    for i in range(1, len(chunks)):
        base_chunk(i)

    lax.fori_loop(1, line, relay, 0)

    def relay2(i, carry):
        pltpu.make_async_copy(a_all.at[0], a_all.at[0], a_recv2.at[i]).wait()
        forward_core(i, 1 - y).start()
        return carry

    lax.fori_loop(0, line, relay2, 0)

    def wait_bytes(ref, sem):
        pltpu.make_async_copy(ref, ref, sem).wait()

    wait_bytes(small_all, s_recv)
    wait_bytes(b_all, b_recv)
    wait_bytes(a_all.at[pl.ds(0, 2 * line)], a_recv3)
    wait_bytes(a_all.at[pl.ds(0, line - 1)], a_send)
    wait_bytes(a_all.at[pl.ds(0, line)], a_send2)
    wait_bytes(a_all.at[pl.ds(0, 2 * line)], a_send3)
    wait_bytes(b_all.at[pl.ds(0, count - 1)], b_send)
    wait_bytes(small_all.at[pl.ds(0, count - 1)], s_send)


def combine_kernel(
    n_grp, n_shard, tok, rank, perturb, step_scale,
    a_ref, b_ref, small_ref, base_ref, pert_ref, upd_ref, weighted,
):
    depth = n_shard // 4
    count, rows, ff = b_ref.shape
    step = pl.program_id(0)
    cand_dev = rows // rank

    @pl.when(step == 0)
    def _():
        fit = small_ref[...][:, :, tok : tok + 1]
        scaled = fit * b_ref[...].astype(F32)
        weighted[...] = scaled.reshape(count * rows, ff).astype(BF16)

    width = upd_ref.shape[1]
    at = pl.ds(pl.multiple_of(step * width, width), width)
    block = a_ref[:, :, at].astype(F32).reshape(count * rows, width).astype(BF16)
    upd_ref[...] = dot_cols(weighted[...], block) * step_scale

    @pl.when(step == 0)
    def _():
        grp = lax.axis_index("grp")
        cols = pert_ref.shape[1]
        picks = [pl.ds(cy * n_grp * depth + grp * depth, depth) for cy in range(4)]
        own_b = jnp.concatenate([b_ref[p].astype(F32) for p in picks], axis=0)
        own_p = jnp.concatenate([small_ref[p] for p in picks], axis=0)
        k = n_shard * rows
        own_b = own_b.reshape(k, ff).astype(BF16)
        own_p = own_p.reshape(k, own_p.shape[2])[:, :tok] * perturb
        high = own_p.astype(BF16)
        low = (own_p - high.astype(F32)).astype(BF16)
        spread = (
            lax.broadcasted_iota(jnp.int32, (tok, cols), 1) % tok
            == lax.broadcasted_iota(jnp.int32, (tok, cols), 0)
        ).astype(F32).astype(BF16)
        r = lax.broadcasted_iota(jnp.int32, (k, cols), 0)
        slab = r // rows
        cy = slab // depth
        sh = (slab % depth) * 4 + (cy % 2) * 2 + cy // 2
        cand = sh * cand_dev + (r % rows) // rank
        keep = cand == lax.broadcasted_iota(jnp.int32, (k, cols), 1) // tok
        wide = lambda v: jnp.where(
            keep, jnp.dot(v, spread, preferred_element_type=F32), 0.0
        ).astype(BF16)
        spread3 = jnp.concatenate([spread, spread, spread], axis=0)
        total = jnp.dot(base_ref[...], spread3, preferred_element_type=F32)
        total = total + dot_cols(own_b, wide(high)) + dot_cols(own_b, wide(low))
        pert_ref[...] = total.astype(BF16)


def local(window, weight, factor_a, factor_b, fitness):
    tok, model_width = window.shape
    cand_dev, rank, _ = factor_a.shape
    n_shard = lax.axis_size("shard")
    n_grp = lax.axis_size("grp")
    total_cands = cand_dev * n_grp * n_shard
    perturb = 0.25 / math.sqrt(model_width)
    step_scale = 0.5 / math.sqrt(total_cands)
    rows = cand_dev * rank
    ff = weight.shape[0]
    half = model_width // n_grp
    count = n_grp * n_shard
    line = n_grp * (n_shard // 4)
    a_rows = factor_a.reshape(rows, model_width)
    b_slabs = factor_b.reshape(rows, n_shard, ff).transpose(1, 0, 2)

    n_chunks = -(-ff // ROW_CHUNK)
    vmem = pl.BlockSpec(memory_space=pltpu.VMEM)
    dma = pltpu.SemaphoreType.DMA
    a_all, b_all, small_all, base = pl.pallas_call(
        functools.partial(exchange_kernel, n_grp, n_shard),
        out_shape=(
            jax.ShapeDtypeStruct((count, rows, half), BF16),
            jax.ShapeDtypeStruct((count, rows, ff), BF16),
            jax.ShapeDtypeStruct((count, rows, 128), F32),
            jax.ShapeDtypeStruct((ff, 3 * tok), BF16),
        ),
        in_specs=[
            pl.BlockSpec(memory_space=pltpu.SMEM), vmem, vmem, vmem,
            pl.BlockSpec(memory_space=pl.ANY),
        ],
        out_specs=(vmem, vmem, vmem, vmem),
        scratch_shapes=[
            pltpu.VMEM((rows, 128), F32),
            pltpu.VMEM((ff, model_width), BF16),
            dma((n_chunks,)),
            dma, dma, dma, dma, dma, dma, dma,
            dma((line,)), dma((line,)), dma,
        ],
        compiler_params=pltpu.CompilerParams(
            collective_id=0, has_side_effects=True, vmem_limit_bytes=60 * 1024 * 1024
        ),
        name="exchange",
    )(fitness, window, a_rows, b_slabs, weight)

    block = min(half, 512)
    cols = n_shard * cand_dev * tok
    whole = lambda shape: pl.BlockSpec(shape, lambda i: (0,) * len(shape))
    perturbed, update = pl.pallas_call(
        functools.partial(combine_kernel, n_grp, n_shard, tok, rank, perturb, step_scale),
        out_shape=(
            jax.ShapeDtypeStruct((ff, cols), BF16),
            jax.ShapeDtypeStruct((ff, half), F32),
        ),
        grid=(half // block,),
        in_specs=[
            vmem, vmem, vmem, vmem,
        ],
        out_specs=(
            whole((ff, cols)),
            pl.BlockSpec((ff, block), lambda i: (0, i)),
        ),
        scratch_shapes=[pltpu.VMEM((count * rows, ff), BF16)],
        compiler_params=pltpu.CompilerParams(vmem_limit_bytes=56 * 1024 * 1024),
        name="combine",
    )(a_all, b_all, small_all, base)
    return perturbed, update


def solution(mesh):
    in_specs = (
        P("grp", None),
        P("shard", None),
        P(("grp", "shard"), None, None),
        P(("grp", "shard"), None, None),
        P(("grp", "shard")),
    )
    out_specs = (P("shard", "grp"), P("shard", "grp"))
    return jax.shard_map(local, mesh=mesh, in_specs=in_specs, out_specs=out_specs, check_vma=False)
```

time: 228 us -> 38.4 us (0.17)
  blocking collectives: 139 us -> 0 us
  local copies, waits for them, and re-layouts: 62.9 us -> 3.49 us
  Pallas kernels: 0 us -> 34 us
  matrix products: 11.5 us -> 0 us
  starting transfers between devices: 7.75 us -> 0 us
  other arithmetic: 4.51 us -> 0 us
    all_gather x6 -> x0, blocking collectives: 105 us -> none  [the longest x4 78.1 us: local(): gathered = lax.all_gather(factor_slab, 'shard', axis=0, tiled=True)]
    unnamed x28 -> x0, local copies, waits for them, and re-layouts: 48.1 us -> none
    unnamed x1 -> x0, blocking collectives: 34 us -> none
    pallas_call x0 -> x2, Pallas kernels: none -> 34 us  [the longest x1 27.8 us: local(): pl.pallas_call(functools.partial(exchange_kernel, n_grp, n_shard), out_sh...]
    all_to_all x2 -> x0, local copies, waits for them, and re-layouts: 12.1 us -> none  [the longest x1 10.7 us: local(): lax.all_to_all(factor_b, 'shard', split_axis=2, concat_axis=0, tiled=True)]
    dot_general x7 -> x0, matrix products: 11.5 us -> none  [the longest x1 4.83 us: local(): lax.dot_general(weight, window, (((1,), (1,)), ((), ())), preferred_eleme...]
    all_to_all x2 -> x0, starting transfers between devices: 7.75 us -> none  [the longest x1 4.23 us: local(): lax.all_to_all(factor_a, 'grp', split_axis=2, concat_axis=0, tiled=True)]
    mul x1 -> x0, other arithmetic: 4.35 us -> none  [local(): update = jnp.concatenate(update_parts, 1) * step_scale]
  transfers between devices with their start and end apart: 2 -> 0, of which waited for: 0 -> 0; matrix products, arithmetic and copies ran while one was open for 17% -> 0% of each run, Pallas kernels for 0% -> 0%
where the time goes in v1:
time: 38.4 us; the launch traced here: 38.1 us
  Pallas kernels  34 us (89%)
  local copies, waits for them, and re-layouts  3.49 us (9%)
  between operations  0.65 us (2%)
    pallas_call x1, Pallas kernels, local(): pl.pallas_call(functools.partial(exchange_kernel, n_grp, n_shard), out_sh...  27.8 us
    pallas_call x1, Pallas kernels, local(): pl.pallas_call(functools.partial(combine_kernel, n_grp, n_shard, tok, ran...  6.18 us
    reshape x2, local copies, waits for them, and re-layouts, local(): b_slabs = factor_b.reshape(rows, n_shard, ff).transpose(1, 0, 2)  2 us
    reshape x1, local copies, waits for them, and re-layouts, local(): a_rows = factor_a.reshape(rows, model_width)  1.49 us

profile of v1, /device:TPU:0, one launch (start us, length us, event | category | flops | bytes accessed | tf_op | source)
XLA Modules:
  0.0 38.1 jit_solution(10996572545179484662)
XLA Ops:
  0.6 1.5 %reshape.10.a_ref = bf16[8,4096]{1,0:T(8,128)(2,1)} reshape(bf16[2,4,4096]{2,1,0:T(4,128)(2,1)} %param.7) | data formatting | bytes 131072 | tf_op jit(solution)/shard_map/reshape | solution.py:270
  2.1 1.3 %reshape.11 = bf16[8,16,688]{2,1,0:T(8,128)(2,1)S(1)} reshape(bf16[2,4,11008]{2,1,0:T(4,128)(2,1)} %param.8) | data formatting | bytes 352256 | tf_op jit(solution)/shard_map/reshape | solution.py:271
  3.4 0.7 %copy.9 = bf16[8,16,688]{2,0,1:T(8,128)(2,1)} copy(bf16[8,16,688]{2,1,0:T(8,128)(2,1)S(1)} %reshape.11) | data formatting | bytes 352256 | tf_op jit(solution)/shard_map/reshape | solution.py:271
  4.1 27.8 %exchange.1 = (bf16[32,8,2048]{2,1,0:T(8,128)(2,1)}, bf16[32,8,688]{2,1,0:T(8,128)(2,1)}, f32[32,8,128]{2,1,0:T(8,128)}, bf16[688,48]{1,0:T(8,128)(2,1)}) custom-call(f32[2]{0:T(128)} %fit_ref.1, bf16[16,4096]{1,0:T(8,128)(2,1)} %win_ref.1, bf16[8,4096]{1,0:T(8,128)(2,1)} %reshape.10.a_ref, bf16[16,8,688]{2,1,0:T(8,128)(2,1)} %bitcast.3, ...), custom_call_target="tpu_custom_call" | custom-call | tf_op jit(solution)/shard_map/exchange/pallas_call | solution.py:276
  31.9 6.2 %combine.1 = (bf16[688,512]{1,0:T(8,128)(2,1)}, f32[688,2048]{1,0:T(8,128)}) custom-call(bf16[32,8,2048]{2,1,0:T(8,128)(2,1)} %get-tuple-element.6.a_ref, bf16[32,8,688]{2,1,0:T(8,128)(2,1)} %get-tuple-element.7.b_ref, f32[32,8,128]{2,1,0:T(8,128)} %get-tuple-element.8.small_ref, bf16[688,48]{1,0:T(8,128)(2,1)} %get-tuple-element.9.base_ref), custom_call_target="tpu_custom_call" | custom-call | tf_op jit(solution)/shard_map/combine/pallas_call | solution.py:305

commit v2 on v1

v2 whole, which is shorter than its diff:
```python
import functools
import math

import jax
import jax.numpy as jnp
from jax import lax
from jax.experimental import pallas as pl
from jax.experimental.pallas import tpu as pltpu
from jax.sharding import PartitionSpec as P

MESH = pl.DeviceIdType.MESH
F32 = jnp.float32
BF16 = jnp.bfloat16
ROW_CHUNK = 128


def dot_rows(left, right):
    return lax.dot_general(left, right, (((1,), (1,)), ((), ())), preferred_element_type=F32)


def dot_cols(left, right):
    return lax.dot_general(left, right, (((0,), (0,)), ((), ())), preferred_element_type=F32)


def exchange_kernel(
    n_grp, n_shard, fit_hbm, win_hbm, a_hbm, b_hbm, weight_ref,
    a_all, b_all, small_all, base_ref,
    fit_ref, win_ref, a_ref, b_ref, in_sem,
    a_rows, b_slabs, small, weight, w_sem, b_send, b_recv, s_send, s_recv,
    a_send, a_send_z, a_send_y, a_send_c, a_recv, a_recv_z, a_recv_y, a_recv_c,
):
    depth = n_shard // 8
    count = n_grp * n_shard
    line = n_grp * depth
    grp = lax.axis_index("grp")
    shard = lax.axis_index("shard")
    core = shard % 2
    y = (shard // 2) % 2
    low_z = (shard // 4) % 2
    high_z = shard // 8
    me = grp * n_shard + shard
    half = a_all.shape[2]
    cand_dev, rank, _ = a_ref.shape
    rows = cand_dev * rank
    ff = weight_ref.shape[0]
    tok = win_ref.shape[0]

    def slot_of(c, yy, lz, i):
        return ((c * 2 + yy) * 2 + lz) * line + i

    own = slot_of(core, y, low_z, grp * depth + high_z)

    inputs = [
        pltpu.make_async_copy(src, dst, in_sem.at[i])
        for i, (src, dst) in enumerate(
            [(a_hbm, a_ref), (b_hbm, b_ref), (win_hbm, win_ref), (fit_hbm, fit_ref)]
        )
    ]
    for load in inputs:
        load.start()

    barrier = pltpu.get_barrier_semaphore()

    def greet(i, carry):
        t = (me + i) % count
        pl.semaphore_signal(
            barrier, inc=1, device_id=(t // n_shard, t % n_shard), device_id_type=MESH
        )
        return carry

    lax.fori_loop(1, count, greet, 0)

    chunks = [(lo, min(ROW_CHUNK, ff - lo)) for lo in range(0, ff, ROW_CHUNK)]
    loads = [
        pltpu.make_async_copy(
            weight_ref.at[pl.ds(lo, size)], weight.at[pl.ds(lo, size)], w_sem.at[i]
        )
        for i, (lo, size) in enumerate(chunks)
    ]
    for load in loads:
        load.start()

    inputs[0].wait()
    a_rows[...] = jnp.concatenate(
        [a_ref[j].astype(F32) for j in range(cand_dev)], axis=0
    ).astype(BF16)
    inputs[1].wait()
    for k in range(n_shard):
        b_slabs[k] = jnp.concatenate(
            [b_ref[j, :, k * ff : (k + 1) * ff].astype(F32) for j in range(cand_dev)], axis=0
        ).astype(BF16)

    pl.semaphore_wait(barrier, count - 1)

    def origin(i):
        g = (grp + n_grp - i // depth) % n_grp
        return g * depth + (high_z + depth - i % depth) % depth

    def a_source(g):
        return a_rows.at[:, pl.ds(pl.multiple_of(g * half, half), half)]

    def send_a(i, carry):
        g = (grp + i // depth) % n_grp
        h = (high_z + i) % depth
        pltpu.make_async_remote_copy(
            src_ref=a_source(g),
            dst_ref=a_all.at[own],
            send_sem=a_send,
            recv_sem=a_recv.at[i],
            device_id=(g, h * 8 + low_z * 4 + y * 2 + core),
            device_id_type=MESH,
        ).start()
        return carry

    lax.fori_loop(1, line, send_a, 0)
    pltpu.make_async_copy(a_source(grp), a_all.at[own], a_recv.at[0]).start()

    def send_b(i, carry):
        t = (me + i) % count
        pltpu.make_async_remote_copy(
            src_ref=b_slabs.at[t % n_shard],
            dst_ref=b_all.at[own],
            send_sem=b_send,
            recv_sem=b_recv,
            device_id=(t // n_shard, t % n_shard),
            device_id_type=MESH,
        ).start()
        return carry

    def forward(slot, c, yy, lz, send_sem, recv_sem):
        pltpu.make_async_remote_copy(
            src_ref=a_all.at[slot],
            dst_ref=a_all.at[slot],
            send_sem=send_sem,
            recv_sem=recv_sem,
            device_id=(grp, high_z * 8 + lz * 4 + yy * 2 + c),
            device_id_type=MESH,
        ).start()

    def wait_bytes(ref, sem):
        pltpu.make_async_copy(ref, ref, sem).wait()

    def relay(i, carry):
        wait_bytes(a_all.at[0], a_recv.at[i])
        slot = slot_of(core, y, low_z, origin(i))
        forward(slot, core, y, 1 - low_z, a_send_z, a_recv_z.at[i])
        forward(slot, core, 1 - y, low_z, a_send_y, a_recv_y.at[i])
        forward(slot, 1 - core, y, low_z, a_send_c, a_recv_c)
        return carry

    def relay_z(i, carry):
        wait_bytes(a_all.at[0], a_recv_z.at[i])
        slot = slot_of(core, y, 1 - low_z, origin(i))
        forward(slot, core, 1 - y, low_z, a_send_y, a_recv_y.at[line + i])
        forward(slot, 1 - core, y, low_z, a_send_c, a_recv_c)
        return carry

    def relay_y(i, carry):
        wait_bytes(a_all.at[0], a_recv_y.at[i])
        lz = (low_z + i // line) % 2
        slot = slot_of(core, 1 - y, lz, origin(i % line))
        forward(slot, 1 - core, y, low_z, a_send_c, a_recv_c)
        return carry

    cuts = [1 + (count - 1) * k // 3 for k in range(4)]
    lax.fori_loop(0, 1, relay, 0)
    lax.fori_loop(cuts[0], cuts[1], send_b, 0)
    pltpu.make_async_copy(b_slabs.at[shard], b_all.at[own], b_recv).start()

    inputs[2].wait()
    inputs[3].wait()
    wide = rows * tok
    win = jnp.concatenate([win_ref[...]] * rows, axis=0)
    projected = dot_rows(a_rows[...], win)
    lane = lax.broadcasted_iota(jnp.int32, (rows, wide), 1)
    row = lax.broadcasted_iota(jnp.int32, (rows, wide), 0)
    small[0:1, :] = jnp.sum(jnp.where(lane // tok == row, projected, 0.0), axis=0, keepdims=True)
    lane = lax.broadcasted_iota(jnp.int32, (1, wide), 1)
    fit = jnp.zeros((1, wide), F32)
    for j in range(cand_dev):
        fit = jnp.where(lane // rank == j, fit_ref[j], fit)
    small[1:2, :] = fit

    def base_chunk(i):
        lo, size = chunks[i]
        loads[i].wait()
        base = dot_rows(weight[pl.ds(lo, size)], win)
        high = base.astype(BF16)
        rest = base - high.astype(F32)
        mid = rest.astype(BF16)
        low = rest - mid.astype(F32)
        part = lax.broadcasted_iota(jnp.int32, base.shape, 1) // tok
        terms = jnp.where(part == 0, high.astype(F32), jnp.where(part == 1, mid.astype(F32), low))
        base_ref[pl.ds(lo, size), :] = jnp.where(part < 3, terms, 0.0).astype(BF16)

    def send_small(i, carry):
        t = (me + i) % count
        pltpu.make_async_remote_copy(
            src_ref=small,
            dst_ref=small_all.at[own],
            send_sem=s_send,
            recv_sem=s_recv,
            device_id=(t // n_shard, t % n_shard),
            device_id_type=MESH,
        ).start()
        return carry

    lax.fori_loop(1, line, relay, 0)
    lax.fori_loop(cuts[1], cuts[2], send_b, 0)
    base_chunk(0)
    lax.fori_loop(0, line, relay_z, 0)
    lax.fori_loop(1, count, send_small, 0)
    pltpu.make_async_copy(small, small_all.at[own], s_recv).start()
    lax.fori_loop(cuts[2], cuts[3], send_b, 0)
    for i in range(1, len(chunks)):
        base_chunk(i)
    lax.fori_loop(0, 2 * line, relay_y, 0)

    wait_bytes(small_all, s_recv)
    wait_bytes(b_all, b_recv)
    wait_bytes(a_all.at[pl.ds(0, 4 * line)], a_recv_c)
    wait_bytes(a_all.at[pl.ds(0, line - 1)], a_send)
    wait_bytes(a_all.at[pl.ds(0, line)], a_send_z)
    wait_bytes(a_all.at[pl.ds(0, 2 * line)], a_send_y)
    wait_bytes(a_all.at[pl.ds(0, 4 * line)], a_send_c)
    wait_bytes(b_all.at[pl.ds(0, count - 1)], b_send)
    wait_bytes(small_all.at[pl.ds(0, count - 1)], s_send)


def combine_kernel(
    n_grp, n_shard, tok, rank, perturb, step_scale,
    a_ref, b_ref, small_ref, base_ref, pert_ref, upd_ref, weighted,
):
    depth = n_shard // 8
    count, rows, ff = b_ref.shape
    wide = small_ref.shape[2]
    step = pl.program_id(0)
    cand_dev = rows // rank

    @pl.when(step == 0)
    def _():
        shape = (count, rows, wide)
        pick = lax.broadcasted_iota(jnp.int32, shape, 2) == lax.broadcasted_iota(jnp.int32, shape, 1)
        fit = jnp.broadcast_to(small_ref[:, 1:2, :], shape)
        fit = jnp.sum(jnp.where(pick, fit, 0.0), axis=2, keepdims=True)
        scaled = fit * b_ref[...].astype(F32)
        weighted[...] = scaled.reshape(count * rows, ff).astype(BF16)

    width = upd_ref.shape[1]
    at = pl.ds(pl.multiple_of(step * width, width), width)
    block = a_ref[:, :, at].astype(F32).reshape(count * rows, width).astype(BF16)
    upd_ref[...] = dot_cols(weighted[...], block) * step_scale

    @pl.when(step == 0)
    def _():
        grp = lax.axis_index("grp")
        cols = pert_ref.shape[1]
        picks = [pl.ds(cyz * n_grp * depth + grp * depth, depth) for cyz in range(8)]
        k = n_shard * rows
        shape = (depth, rows, wide)
        keep = (
            lax.broadcasted_iota(jnp.int32, shape, 2) // tok
            == lax.broadcasted_iota(jnp.int32, shape, 1)
        )
        own_b = jnp.concatenate([b_ref[p].astype(F32) for p in picks], axis=0)
        own_p = jnp.concatenate(
            [
                jnp.where(keep, jnp.broadcast_to(small_ref[p, 0:1, :], shape) * perturb, 0.0)
                for p in picks
            ],
            axis=0,
        )
        own_b = own_b.reshape(k, ff).astype(BF16)
        own_p = own_p.reshape(k, wide)
        high = own_p.astype(BF16)
        low = (own_p - high.astype(F32)).astype(BF16)
        spread = (
            lax.broadcasted_iota(jnp.int32, (wide, cols), 1) % tok
            == lax.broadcasted_iota(jnp.int32, (wide, cols), 0) % tok
        ).astype(F32).astype(BF16)
        r = lax.broadcasted_iota(jnp.int32, (k, cols), 0)
        slab = r // rows
        cyz = slab // depth
        sh = (slab % depth) * 8 + (cyz % 2) * 4 + (cyz // 2 % 2) * 2 + cyz // 4
        cand = sh * cand_dev + (r % rows) // rank
        mine = cand == lax.broadcasted_iota(jnp.int32, (k, cols), 1) // tok

        def blocks(v):
            return jnp.where(mine, jnp.dot(v, spread, preferred_element_type=F32), 0.0).astype(BF16)

        total = jnp.dot(base_ref[...], spread, preferred_element_type=F32)
        total = total + dot_cols(own_b, blocks(high)) + dot_cols(own_b, blocks(low))
        pert_ref[...] = total.astype(BF16)


def local(window, weight, factor_a, factor_b, fitness):
    tok, model_width = window.shape
    cand_dev, rank, _ = factor_a.shape
    n_shard = lax.axis_size("shard")
    n_grp = lax.axis_size("grp")
    total_cands = cand_dev * n_grp * n_shard
    perturb = 0.25 / math.sqrt(model_width)
    step_scale = 0.5 / math.sqrt(total_cands)
    rows = cand_dev * rank
    ff = weight.shape[0]
    half = model_width // n_grp
    count = n_grp * n_shard
    line = n_grp * (n_shard // 8)
    wide = rows * tok

    operands = (fitness, window, factor_a, factor_b, weight)
    n_chunks = -(-ff // ROW_CHUNK)
    vmem = pl.BlockSpec(memory_space=pltpu.VMEM)
    dma = pltpu.SemaphoreType.DMA
    a_all, b_all, small_all, base = pl.pallas_call(
        functools.partial(exchange_kernel, n_grp, n_shard),
        out_shape=(
            jax.ShapeDtypeStruct((count, rows, half), BF16),
            jax.ShapeDtypeStruct((count, rows, ff), BF16),
            jax.ShapeDtypeStruct((count, 2, wide), F32),
            jax.ShapeDtypeStruct((ff, wide), BF16),
        ),
        in_specs=[pl.BlockSpec(memory_space=pltpu.HBM)] * 5,
        out_specs=(vmem, vmem, vmem, vmem),
        scratch_shapes=[
            pltpu.SMEM(fitness.shape, F32),
            pltpu.VMEM(window.shape, BF16),
            pltpu.VMEM(factor_a.shape, BF16),
            pltpu.VMEM(factor_b.shape, BF16),
            dma((4,)),
            pltpu.VMEM((rows, model_width), BF16),
            pltpu.VMEM((n_shard, rows, ff), BF16),
            pltpu.VMEM((2, wide), F32),
            pltpu.VMEM((ff, model_width), BF16),
            dma((n_chunks,)),
            dma, dma, dma, dma, dma, dma, dma, dma,
            dma((line,)), dma((line,)), dma((2 * line,)), dma,
        ],
        compiler_params=pltpu.CompilerParams(
            collective_id=0, has_side_effects=True, vmem_limit_bytes=50 * 1024 * 1024
        ),
        name="exchange",
    )(*[pltpu.with_memory_space_constraint(v, pltpu.HBM) for v in operands])

    block = min(half, 512)
    cols = n_shard * cand_dev * tok
    whole = lambda shape: pl.BlockSpec(shape, lambda i: (0,) * len(shape))
    perturbed, update = pl.pallas_call(
        functools.partial(combine_kernel, n_grp, n_shard, tok, rank, perturb, step_scale),
        out_shape=(
            jax.ShapeDtypeStruct((ff, cols), BF16),
            jax.ShapeDtypeStruct((ff, half), F32),
        ),
        grid=(half // block,),
        in_specs=[
            vmem, vmem, vmem, vmem,
        ],
        out_specs=(
            whole((ff, cols)),
            pl.BlockSpec((ff, block), lambda i: (0, i)),
        ),
        scratch_shapes=[pltpu.VMEM((count * rows, ff), BF16)],
        compiler_params=pltpu.CompilerParams(vmem_limit_bytes=40 * 1024 * 1024),
        name="combine",
    )(a_all, b_all, small_all, base)
    return perturbed, update


def solution(mesh):
    in_specs = (
        P("grp", None),
        P("shard", None),
        P(("grp", "shard"), None, None),
        P(("grp", "shard"), None, None),
        P(("grp", "shard")),
    )
    out_specs = (P("shard", "grp"), P("shard", "grp"))
    return jax.shard_map(local, mesh=mesh, in_specs=in_specs, out_specs=out_specs, check_vma=False)
```

time: 38.4 us -> 28.7 us (0.75)
  Pallas kernels: 34 us -> 27.9 us
  local copies, waits for them, and re-layouts: 3.49 us -> 0 us
    pallas_call x1, Pallas kernels: 27.8 us -> 23.1 us  [local(): pl.pallas_call(functools.partial(exchange_kernel, n_grp, n_shard), out_sh...]
    reshape x3 -> x0, local copies, waits for them, and re-layouts: 3.49 us -> none  [the longest x2 2 us: local(): b_slabs = factor_b.reshape(rows, n_shard, ff).transpose(1, 0, 2)]
    pallas_call x1, Pallas kernels: 6.18 us -> 4.81 us  [local(): pl.pallas_call(functools.partial(combine_kernel, n_grp, n_shard, tok, ran...]
where the time goes in v2:
time: 28.7 us; the launch traced here: 28.5 us
  Pallas kernels  27.9 us (97%)
  between operations  0.64 us (2%)
    pallas_call x1, Pallas kernels, local(): pl.pallas_call(functools.partial(exchange_kernel, n_grp, n_shard), out_sh...  23.1 us
    pallas_call x1, Pallas kernels, local(): pl.pallas_call(functools.partial(combine_kernel, n_grp, n_shard, tok, ran...  4.81 us

profile of v2, /device:TPU:0, one launch (start us, length us, event | category | flops | bytes accessed | tf_op | source)
XLA Modules:
  0.0 28.5 jit_solution(3329311341551974675)
XLA Ops:
  0.6 23.1 %exchange.1 = (bf16[32,8,2048]{2,1,0:T(8,128)(2,1)S(1)}, bf16[32,8,688]{2,1,0:T(8,128)(2,1)S(1)}, f32[32,2,128]{2,1,0:T(2,128)S(1)}, bf16[688,128]{1,0:T(8,128)(2,1)S(1)}) custom-call(f32[2]{0:T(128)} %fit_hbm.1, bf16[16,4096]{1,0:T(8,128)(2,1)} %win_hbm.1, bf16[2,4,4096]{2,1,0:T(4,128)(2,1)} %a_hbm.1, bf16[2,4,11008]{2,1,0:T(4,128)(2,1)} %b_hbm.1, ...), custom_call_target="tpu_custom_call" | custom-call | tf_op jit(solution)/shard_map/exchange/pallas_call | solution.py:315
  23.7 4.8 %combine.1 = (bf16[688,512]{1,0:T(8,128)(2,1)}, f32[688,2048]{1,0:T(8,128)}) custom-call(bf16[32,8,2048]{2,1,0:T(8,128)(2,1)S(1)} %get-tuple-element.6.a_ref, bf16[32,8,688]{2,1,0:T(8,128)(2,1)S(1)} %get-tuple-element.7.b_ref, f32[32,2,128]{2,1,0:T(2,128)S(1)} %get-tuple-element.8.small_ref, bf16[688,128]{1,0:T(8,128)(2,1)S(1)} %get-tuple-element.9.base_ref), custom_call_target="tpu_custom_call" | custom-call | tf_op jit(solution)/shard_map/combine/pallas_call | solution.py:348

commit v3 on v2

--- a/solution.py
+++ b/solution.py
@@ -26,7 +26,7 @@
     n_grp, n_shard, fit_hbm, win_hbm, a_hbm, b_hbm, weight_ref,
     a_all, b_all, small_all, base_ref,
     fit_ref, win_ref, a_ref, b_ref, in_sem,
-    a_rows, b_slabs, small, weight, w_sem, b_send, b_recv, s_send, s_recv,
+    a_rows, b_slabs, small, weight, w_sem, b_send, b_recv, b_send_x, b_recv_x, s_send, s_recv,
     a_send, a_send_z, a_send_y, a_send_c, a_recv, a_recv_z, a_recv_y, a_recv_c,
 ):
     depth = n_shard // 8
@@ -46,9 +46,12 @@
     tok = win_ref.shape[0]
 
     def slot_of(c, yy, lz, i):
-        return ((c * 2 + yy) * 2 + lz) * line + i
-
-    own = slot_of(core, y, low_z, grp * depth + high_z)
+        return i // depth * n_shard + ((c * 2 + yy) * 2 + lz) * depth + i % depth
+
+    def slot_at(s):
+        return slot_of(s % 2, s // 2 % 2, s // 4 % 2, grp * depth + s // 8)
+
+    own = slot_at(shard)
 
     inputs = [
         pltpu.make_async_copy(src, dst, in_sem.at[i])
@@ -116,15 +119,35 @@
     pltpu.make_async_copy(a_source(grp), a_all.at[own], a_recv.at[0]).start()
 
     def send_b(i, carry):
-        t = (me + i) % count
+        to = (shard + i) % n_shard
         pltpu.make_async_remote_copy(
-            src_ref=b_slabs.at[t % n_shard],
+            src_ref=b_slabs.at[to],
             dst_ref=b_all.at[own],
             send_sem=b_send,
-            recv_sem=b_recv,
-            device_id=(t // n_shard, t % n_shard),
+            recv_sem=b_recv.at[i],
+            device_id=(grp, to),
             device_id_type=MESH,
         ).start()
+        return carry
+
+    def cross_b(src, slot):
+        def one(k, carry):
+            pltpu.make_async_remote_copy(
+                src_ref=src,
+                dst_ref=b_all.at[slot],
+                send_sem=b_send_x,
+                recv_sem=b_recv_x,
+                device_id=((grp + k) % n_grp, shard),
+                device_id_type=MESH,
+            ).start()
+            return carry
+
+        lax.fori_loop(1, n_grp, one, 0)
+
+    def relay_b(i, carry):
+        wait_bytes(b_all.at[0], b_recv.at[i])
+        slot = slot_at((shard + n_shard - i) % n_shard)
+        cross_b(b_all.at[slot], slot)
         return carry
 
     def forward(slot, c, yy, lz, send_sem, recv_sem):
@@ -162,10 +185,10 @@
         forward(slot, 1 - core, y, low_z, a_send_c, a_recv_c)
         return carry
 
-    cuts = [1 + (count - 1) * k // 3 for k in range(4)]
     lax.fori_loop(0, 1, relay, 0)
-    lax.fori_loop(cuts[0], cuts[1], send_b, 0)
-    pltpu.make_async_copy(b_slabs.at[shard], b_all.at[own], b_recv).start()
+    cross_b(b_slabs.at[shard], own)
+    pltpu.make_async_copy(b_slabs.at[shard], b_all.at[own], b_recv.at[0]).start()
+    lax.fori_loop(1, n_shard, send_b, 0)
 
     inputs[2].wait()
     inputs[3].wait()
@@ -206,24 +229,27 @@
         return carry
 
     lax.fori_loop(1, line, relay, 0)
-    lax.fori_loop(cuts[1], cuts[2], send_b, 0)
-    base_chunk(0)
+    for i in range(0, 1):
+        base_chunk(i)
+    lax.fori_loop(1, n_shard // 2, relay_b, 0)
     lax.fori_loop(0, line, relay_z, 0)
     lax.fori_loop(1, count, send_small, 0)
     pltpu.make_async_copy(small, small_all.at[own], s_recv).start()
-    lax.fori_loop(cuts[2], cuts[3], send_b, 0)
+    lax.fori_loop(n_shard // 2, n_shard, relay_b, 0)
     for i in range(1, len(chunks)):
         base_chunk(i)
     lax.fori_loop(0, 2 * line, relay_y, 0)
 
     wait_bytes(small_all, s_recv)
-    wait_bytes(b_all, b_recv)
+    wait_bytes(b_all.at[0], b_recv.at[0])
+    wait_bytes(b_all.at[pl.ds(0, count - n_shard)], b_recv_x)
+    wait_bytes(b_all.at[pl.ds(0, count - n_shard)], b_send_x)
     wait_bytes(a_all.at[pl.ds(0, 4 * line)], a_recv_c)
     wait_bytes(a_all.at[pl.ds(0, line - 1)], a_send)
     wait_bytes(a_all.at[pl.ds(0, line)], a_send_z)
     wait_bytes(a_all.at[pl.ds(0, 2 * line)], a_send_y)
     wait_bytes(a_all.at[pl.ds(0, 4 * line)], a_send_c)
-    wait_bytes(b_all.at[pl.ds(0, count - 1)], b_send)
+    wait_bytes(b_all.at[pl.ds(0, n_shard - 1)], b_send)
     wait_bytes(small_all.at[pl.ds(0, count - 1)], s_send)
 
 
@@ -255,21 +281,16 @@
     def _():
         grp = lax.axis_index("grp")
         cols = pert_ref.shape[1]
-        picks = [pl.ds(cyz * n_grp * depth + grp * depth, depth) for cyz in range(8)]
+        mine = pl.ds(grp * n_shard, n_shard)
         k = n_shard * rows
-        shape = (depth, rows, wide)
+        shape = (n_shard, rows, wide)
         keep = (
             lax.broadcasted_iota(jnp.int32, shape, 2) // tok
             == lax.broadcasted_iota(jnp.int32, shape, 1)
         )
-        own_b = jnp.concatenate([b_ref[p].astype(F32) for p in picks], axis=0)
-        own_p = jnp.concatenate(
-            [
-                jnp.where(keep, jnp.broadcast_to(small_ref[p, 0:1, :], shape) * perturb, 0.0)
-                for p in picks
-            ],
-            axis=0,
-        )
+        own_b = b_ref[mine].astype(F32)
+        own_p = jnp.broadcast_to(small_ref[mine, 0:1, :], shape) * perturb
+        own_p = jnp.where(keep, own_p, 0.0)
         own_b = own_b.reshape(k, ff).astype(BF16)
         own_p = own_p.reshape(k, wide)
         high = own_p.astype(BF16)
@@ -283,10 +304,10 @@
         cyz = slab // depth
         sh = (slab % depth) * 8 + (cyz % 2) * 4 + (cyz // 2 % 2) * 2 + cyz // 4
         cand = sh * cand_dev + (r % rows) // rank
-        mine = cand == lax.broadcasted_iota(jnp.int32, (k, cols), 1) // tok
+        same = cand == lax.broadcasted_iota(jnp.int32, (k, cols), 1) // tok
 
         def blocks(v):
-            return jnp.where(mine, jnp.dot(v, spread, preferred_element_type=F32), 0.0).astype(BF16)
+            return jnp.where(same, jnp.dot(v, spread, preferred_element_type=F32), 0.0).astype(BF16)
 
         total = jnp.dot(base_ref[...], spread, preferred_element_type=F32)
         total = total + dot_cols(own_b, blocks(high)) + dot_cols(own_b, blocks(low))
@@ -333,7 +354,7 @@
             pltpu.VMEM((2, wide), F32),
             pltpu.VMEM((ff, model_width), BF16),
             dma((n_chunks,)),
-            dma, dma, dma, dma, dma, dma, dma, dma,
+            dma, dma((n_shard,)), dma, dma, dma, dma, dma, dma, dma, dma,
             dma((line,)), dma((line,)), dma((2 * line,)), dma,
         ],
         compiler_params=pltpu.CompilerParams(

time: 28.7 us -> 27.5 us (0.958)
  Pallas kernels: 27.9 us -> 26.7 us
    pallas_call x1, Pallas kernels: 23.1 us -> 21.9 us  [local(): pl.pallas_call(functools.partial(exchange_kernel, n_grp, n_shard), out_sh...]
where the time goes in v3:
time: 27.5 us; the launch traced here: 27.3 us
  Pallas kernels  26.7 us (97%)
  between operations  0.64 us (2%)
    pallas_call x1, Pallas kernels, local(): pl.pallas_call(functools.partial(exchange_kernel, n_grp, n_shard), out_sh...  21.9 us
    pallas_call x1, Pallas kernels, local(): pl.pallas_call(functools.partial(combine_kernel, n_grp, n_shard, tok, ran...  4.8 us

profile of v3, /device:TPU:0, one launch (start us, length us, event | category | flops | bytes accessed | tf_op | source)
XLA Modules:
  0.0 27.3 jit_solution(14386976830494898170)
XLA Ops:
  0.6 21.9 %exchange.1 = (bf16[32,8,2048]{2,1,0:T(8,128)(2,1)S(1)}, bf16[32,8,688]{2,1,0:T(8,128)(2,1)S(1)}, f32[32,2,128]{2,1,0:T(2,128)S(1)}, bf16[688,128]{1,0:T(8,128)(2,1)S(1)}) custom-call(f32[2]{0:T(128)} %fit_hbm.1, bf16[16,4096]{1,0:T(8,128)(2,1)} %win_hbm.1, bf16[2,4,4096]{2,1,0:T(4,128)(2,1)} %a_hbm.1, bf16[2,4,11008]{2,1,0:T(4,128)(2,1)} %b_hbm.1, ...), custom_call_target="tpu_custom_call" | custom-call | tf_op jit(solution)/shard_map/exchange/pallas_call | solution.py:336
  22.5 4.8 %combine.1 = (bf16[688,512]{1,0:T(8,128)(2,1)}, f32[688,2048]{1,0:T(8,128)}) custom-call(bf16[32,8,2048]{2,1,0:T(8,128)(2,1)S(1)} %get-tuple-element.6.a_ref, bf16[32,8,688]{2,1,0:T(8,128)(2,1)S(1)} %get-tuple-element.7.b_ref, f32[32,2,128]{2,1,0:T(2,128)S(1)} %get-tuple-element.8.small_ref, bf16[688,128]{1,0:T(8,128)(2,1)S(1)} %get-tuple-element.9.base_ref), custom_call_target="tpu_custom_call" | custom-call | tf_op jit(solution)/shard_map/combine/pallas_call | solution.py:369

commit v4 on v3

--- a/solution.py
+++ b/solution.py
@@ -363,7 +363,7 @@
         name="exchange",
     )(*[pltpu.with_memory_space_constraint(v, pltpu.HBM) for v in operands])
 
-    block = min(half, 512)
+    block = min(half, 1024)
     cols = n_shard * cand_dev * tok
     whole = lambda shape: pl.BlockSpec(shape, lambda i: (0,) * len(shape))
     perturbed, update = pl.pallas_call(

time: 27.5 us -> 27.1 us (0.985)
  Pallas kernels: 26.7 us -> 26.4 us
    pallas_call x1, Pallas kernels: 4.8 us -> 4.46 us  [local(): pl.pallas_call(functools.partial(combine_kernel, n_grp, n_shard, tok, ran...]
where the time goes in v4:
time: 27.1 us; the launch traced here: 27 us
  Pallas kernels  26.4 us (97%)
  between operations  0.64 us (2%)
    pallas_call x1, Pallas kernels, local(): pl.pallas_call(functools.partial(exchange_kernel, n_grp, n_shard), out_sh...  21.9 us
    pallas_call x1, Pallas kernels, local(): pl.pallas_call(functools.partial(combine_kernel, n_grp, n_shard, tok, ran...  4.46 us

profile of v4, /device:TPU:0, one launch (start us, length us, event | category | flops | bytes accessed | tf_op | source)
XLA Modules:
  0.0 27.0 jit_solution(5628582341943467212)
XLA Ops:
  0.6 21.9 %exchange.1 = (bf16[32,8,2048]{2,1,0:T(8,128)(2,1)S(1)}, bf16[32,8,688]{2,1,0:T(8,128)(2,1)S(1)}, f32[32,2,128]{2,1,0:T(2,128)S(1)}, bf16[688,128]{1,0:T(8,128)(2,1)S(1)}) custom-call(f32[2]{0:T(128)} %fit_hbm.1, bf16[16,4096]{1,0:T(8,128)(2,1)} %win_hbm.1, bf16[2,4,4096]{2,1,0:T(4,128)(2,1)} %a_hbm.1, bf16[2,4,11008]{2,1,0:T(4,128)(2,1)} %b_hbm.1, ...), custom_call_target="tpu_custom_call" | custom-call | tf_op jit(solution)/shard_map/exchange/pallas_call | solution.py:336
  22.5 4.5 %combine.1 = (bf16[688,512]{1,0:T(8,128)(2,1)}, f32[688,2048]{1,0:T(8,128)}) custom-call(bf16[32,8,2048]{2,1,0:T(8,128)(2,1)S(1)} %get-tuple-element.6.a_ref, bf16[32,8,688]{2,1,0:T(8,128)(2,1)S(1)} %get-tuple-element.7.b_ref, f32[32,2,128]{2,1,0:T(2,128)S(1)} %get-tuple-element.8.small_ref, bf16[688,128]{1,0:T(8,128)(2,1)S(1)} %get-tuple-element.9.base_ref), custom_call_target="tpu_custom_call" | custom-call | tf_op jit(solution)/shard_map/combine/pallas_call | solution.py:369
